TPU v7x, 32 devices: a whole 2x2x4 slice. The times are simulated.
32 devices in a mesh: section: 4 (over x, core), tensor: 4 (over z), dp: 2 (over y).
Axes of the slice: x: 2, y: 2, z: 4, core: 2. Of those that a mesh axis runs over, the one named last changes fastest.
Arguments:
- layer_in: bfloat16 [2, 2, 4, 2, 128, 2560], P(None, None, 'section', 'dp', 'tensor'), may hold values from -6 to 6
- carry_in: bfloat16 [2, 4, 2, 128, 2560], P(None, 'section', 'dp', 'tensor'), may hold values from -6 to 6
- top_grad: bfloat16 [1, 2, 128, 2560], P(None, 'dp', 'tensor'), may hold values from -6 to 6
- w_qkv: bfloat16 [2, 4, 2560, 2560], P(None, 'section', None, 'tensor'), may hold values from -1 to 1
- w_out: bfloat16 [2, 4, 2048, 2560], P(None, 'section', 'tensor'), may hold values from -0.125 to 0.125
- gain: float32 [2, 4, 2560], P(None, 'section'), may hold values from 0.5 to 1.5
Outputs:
- unit_grads: bfloat16 [2, 2, 4, 2, 128, 2560], P(None, None, 'section', 'dp', 'tensor')
- grad_qkv: bfloat16 [2, 4, 2560, 2560], P(None, 'section', 'dp', 'tensor')
- grad_out: bfloat16 [2, 4, 2048, 2560], P(None, 'section', ('tensor', 'dp'))
- grad_gain: float32 [2, 4, 2560], P(None, 'section')
All inputs are finite; a program needn't handle non-finite values.
Results may differ from a plain program's by a relative error of at most 0.022.
The roundings to bfloat16 on the way count: a program that leaves them out, or rounds other values in their place, can miss the bound.
Values may be sent and summed in bfloat16 or wider, within the bound.
A program may use at most 128 MiB of HBM per device.

v0:
```python
import math
import jax
import jax.numpy as jnp
from jax import lax
from jax.sharding import PartitionSpec as P

KV = 4
HD = 64
GROUP = 8
epsilon = 1e-06
rope_base = 1000000.0


def from_behind(value, axis, steps):
    count = lax.axis_size(axis)
    first, last = (max(0, -steps), min(count, count - steps))
    return lax.ppermute(value, axis, [(source, source + steps) for source in range(first, last)])


def rope_tables(length, head_width):
    half_width = head_width // 2
    exponent = jnp.arange(half_width, dtype=jnp.float32) * (2.0 / head_width)
    frequency = rope_base ** (-exponent)
    angle = jnp.arange(length, dtype=jnp.float32)[:, None] * frequency[None, :]
    return (jnp.cos(angle), jnp.sin(angle))


def rotate(values, cosine_table, sine_table, direction):
    half_width = values.shape[-1] // 2
    table_shape = (values.shape[0],) + (1,) * (values.ndim - 2) + (half_width,)
    cosine = cosine_table.reshape(table_shape)
    sine_part = direction * sine_table.reshape(table_shape)
    lower_half = values[..., :half_width]
    upper_half = values[..., half_width:]
    return jnp.concatenate(
        [
            lower_half * cosine - upper_half * sine_part,
            upper_half * cosine + lower_half * sine_part,
        ],
        axis=-1,
    )


def local(layer_in, carry_in, top_grad, w_qkv, w_out, gain):
    ticks = layer_in.shape[0]
    own_rows = layer_in.shape[4]
    length = own_rows * lax.axis_size("tensor")
    kv_local = KV // lax.axis_size("tensor")
    section_index = lax.axis_index("section")
    at_first = section_index == 0
    at_last = section_index == lax.axis_size("section") - 1
    cosine_table, sine_table = rope_tables(length, HD)
    score_scale = 1.0 / math.sqrt(HD)
    causal_mask = jnp.arange(length)[:, None] >= jnp.arange(length)[None, :]
    layer_rows = layer_in[:, :, 0, 0]
    carried = carry_in[:, 0, 0]
    fresh_grads = top_grad[:, 0]
    weight_qkv = w_qkv[:, 0]
    weight_out = w_out[:, 0]
    gain_rows = gain[:, 0]
    contract_rows = (((0,), (0,)), ((), ()))
    contract_cols = (((1,), (1,)), ((), ()))
    qkv_sums = [
        jnp.zeros(weight_qkv.shape[1:], jnp.float32),
        jnp.zeros(weight_qkv.shape[1:], jnp.float32),
    ]
    out_sums = [
        jnp.zeros(weight_out.shape[1:], jnp.float32),
        jnp.zeros(weight_out.shape[1:], jnp.float32),
    ]
    gain_totals = [
        jnp.zeros(gain_rows.shape[1:], jnp.float32),
        jnp.zeros(gain_rows.shape[1:], jnp.float32),
    ]

    def apply_weights(member, stored):
        normed, grad_full, attended, grad_projected = stored
        qkv_sums[member] = qkv_sums[member] + lax.dot_general(
            normed, grad_projected, contract_rows, preferred_element_type=jnp.float32
        )
        out_sums[member] = out_sums[member] + lax.dot_general(
            attended, grad_full, contract_rows, preferred_element_type=jnp.float32
        )

    inputs = [carried[0], carried[1]]
    per_tick = []
    for position in range(ticks):
        outcome = [None, None]
        pending_members = []
        pending_saved = []
        for member in (1, 0):
            layer_part = layer_rows[position, member]
            grad_output = inputs[member]
            inputs_float = layer_part.astype(jnp.float32)
            inverse = lax.rsqrt(
                jnp.mean(inputs_float * inputs_float, axis=-1, keepdims=True) + epsilon
            )
            unit_rows = inputs_float * inverse
            normed_own = (unit_rows * gain_rows[member]).astype(jnp.bfloat16)
            input_normed = lax.all_gather(normed_own, "tensor", axis=0, tiled=True)
            input_grad_full = lax.all_gather(grad_output, "tensor", axis=0, tiled=True)
            projected = jnp.dot(
                input_normed, weight_qkv[member], preferred_element_type=jnp.float32
            )
            projected = projected.reshape(length, kv_local, GROUP + 2, HD)
            query_rot = rotate(projected[:, :, :GROUP], cosine_table, sine_table, 1.0).astype(
                jnp.bfloat16
            )
            key_rot = rotate(projected[:, :, GROUP], cosine_table, sine_table, 1.0).astype(
                jnp.bfloat16
            )
            value_rows = projected[:, :, GROUP + 1].astype(jnp.bfloat16)
            scores = (
                jnp.einsum("tkgd,ukd->kgtu", query_rot, key_rot, preferred_element_type=jnp.float32)
                * score_scale
            )
            scores = jnp.where(causal_mask, scores, -1e30)
            exponentials = jnp.exp(scores - jnp.max(scores, axis=-1, keepdims=True))
            softmax_rows = exponentials / jnp.sum(exponentials, axis=-1, keepdims=True)
            softmax_low = softmax_rows.astype(jnp.bfloat16)
            input_attended = jnp.einsum(
                "kgtu,ukd->tkgd", softmax_low, value_rows, preferred_element_type=jnp.float32
            )
            input_attended = input_attended.astype(jnp.bfloat16).reshape(
                length, kv_local * GROUP * HD
            )
            grad_attended = lax.dot_general(
                input_grad_full,
                weight_out[member],
                contract_cols,
                preferred_element_type=jnp.float32,
            ).astype(jnp.bfloat16)
            grad_heads = grad_attended.reshape(length, kv_local, GROUP, HD)
            grad_softmax = jnp.einsum(
                "tkgd,ukd->kgtu", grad_heads, value_rows, preferred_element_type=jnp.float32
            )
            row_total = jnp.sum(softmax_rows * grad_softmax, axis=-1, keepdims=True)
            grad_scores = (softmax_rows * (grad_softmax - row_total) * score_scale).astype(
                jnp.bfloat16
            )
            grad_value = jnp.einsum(
                "kgtu,tkgd->ukd", softmax_low, grad_heads, preferred_element_type=jnp.float32
            )
            grad_query = rotate(
                jnp.einsum(
                    "kgtu,ukd->tkgd", grad_scores, key_rot, preferred_element_type=jnp.float32
                ),
                cosine_table,
                sine_table,
                -1.0,
            )
            grad_key = rotate(
                jnp.einsum(
                    "kgtu,tkgd->ukd", grad_scores, query_rot, preferred_element_type=jnp.float32
                ),
                cosine_table,
                sine_table,
                -1.0,
            )
            input_grad_projected = jnp.concatenate(
                [grad_query, grad_key[:, :, None], grad_value[:, :, None]], axis=2
            )
            input_grad_projected = input_grad_projected.reshape(
                length, kv_local * (GROUP + 2) * HD
            ).astype(jnp.bfloat16)
            grad_normed = lax.psum_scatter(
                lax.dot_general(
                    input_grad_projected,
                    weight_qkv[member],
                    contract_cols,
                    preferred_element_type=jnp.float32,
                ).astype(jnp.bfloat16),
                "tensor",
                scatter_dimension=0,
                tiled=True,
            ).astype(jnp.float32)
            grad_unit = grad_normed * gain_rows[member]
            grad_rows = inverse * (
                grad_unit - unit_rows * jnp.mean(grad_unit * unit_rows, axis=-1, keepdims=True)
            )
            grad_input = (grad_output.astype(jnp.float32) + grad_rows).astype(jnp.bfloat16)
            grad_scale = jnp.sum(grad_normed * unit_rows, axis=0)
            grad_input, stored, grad_scale = (
                grad_input,
                (input_normed, input_grad_full, input_attended, input_grad_projected),
                grad_scale,
            )
            outcome[member] = grad_input
            gain_totals[member] = gain_totals[member] + grad_scale
            pending_members.append(member)
            pending_saved.append(stored)
        if position + 1 < ticks:
            upward = from_behind(outcome[1], "section", 1)
            downward = from_behind(outcome[0], "section", -1)
            pending_saved, upward, downward = lax.optimization_barrier(
                (pending_saved, upward, downward)
            )
            inputs = [
                jnp.where(at_last, outcome[1], downward),
                jnp.where(at_first, fresh_grads[position], upward),
            ]
        for member, stored in zip(pending_members, pending_saved):
            apply_weights(member, stored)
        per_tick.append(jnp.stack(outcome))
    grad_qkv_all, grad_out_all = (
        lax.psum_scatter(
            jnp.stack(qkv_sums).astype(jnp.bfloat16), "dp", scatter_dimension=1, tiled=True
        ).astype(jnp.float32),
        lax.psum_scatter(
            jnp.stack(out_sums).astype(jnp.bfloat16), "dp", scatter_dimension=1, tiled=True
        ).astype(jnp.float32),
    )
    gain_total = lax.psum(jnp.stack(gain_totals), ("tensor", "dp"))
    unit_grads = jnp.stack(per_tick)[:, :, None, None]
    return (
        unit_grads,
        grad_qkv_all.astype(jnp.bfloat16)[:, None],
        grad_out_all.astype(jnp.bfloat16)[:, None],
        gain_total[:, None],
    )


def solution(mesh):
    in_specs = (
        P(None, None, "section", "dp", "tensor", None),
        P(None, "section", "dp", "tensor", None),
        P(None, "dp", "tensor", None),
        P(None, "section", None, "tensor"),
        P(None, "section", "tensor", None),
        P(None, "section", None),
    )
    out_specs = (
        P(None, None, "section", "dp", "tensor", None),
        P(None, "section", "dp", "tensor"),
        P(None, "section", ("tensor", "dp"), None),
        P(None, "section", None),
    )
    return jax.shard_map(local, mesh=mesh, in_specs=in_specs, out_specs=out_specs, check_vma=False)
```

profile of v0, /device:TPU:0, one launch (start us, length us, event | category | flops | bytes accessed | tf_op | source)
XLA Modules:
  0.0 479.4 jit_solution(15156333436391977317)
XLA Ops:
  11.8 19.7 %all-gather = bf16[1,1,1,128,2560]{4,3,2,1,0:T(8,128)(2,1)S(1)} all-gather(bf16[1,1,1,32,2560]{4,3,2,1,0:T(8,128)(2,1)S(1)} %get-tuple-element.68), channel_id=2, replica_groups=mesh['section'=4,'tensor'=4,'dp'=2] {'tensor'}, dimensions={3}, use_global_device_ids=true | all-gather | bytes 819200 | tf_op jit(solution)/shard_map/all_gather | solution.py:101
  35.4 17.5 %all_gather.24 = bf16[128,2560]{1,0:T(8,128)(2,1)} all-gather(bf16[32,2560]{1,0:T(8,128)(2,1)S(1)} %get-tuple-element.58), channel_id=1, replica_groups=mesh['section'=4,'tensor'=4,'dp'=2] {'tensor'}, dimensions={0}, use_global_device_ids=true | all-gather | bytes 819200 | tf_op jit(solution)/shard_map/all_gather | solution.py:100
  52.9 16.7 %all_gather.26 = bf16[128,2560]{1,0:T(8,128)(2,1)} all-gather(bf16[32,2560]{1,0:T(8,128)(2,1)S(1)} %get-tuple-element.59), channel_id=1, replica_groups=mesh['section'=4,'tensor'=4,'dp'=2] {'tensor'}, dimensions={0}, use_global_device_ids=true | all-gather | bytes 819200 | tf_op jit(solution)/shard_map/all_gather | solution.py:100
  69.6 6.2 %slice_bitcast_fusion.1 = (bf16[640,2560]{0,1:T(8,128)(2,1)}, bf16[640,2560]{0,1:T(8,128)(2,1)}) fusion(bf16[2,1,2560,640]{3,2,1,0:T(8,128)(2,1)} %param.9), kind=kLoop, calls=%fused_computation.30 | loop fusion | bytes 13107200 | tf_op jit(solution)/shard_map/dot_general | solution.py:102
  75.9 4.0 copy.39
  82.7 5.7 %copy.44 = bf16[640,2560]{1,0:T(8,128)(2,1)} copy(bf16[640,2560]{0,1:T(8,128)(2,1)} %get-tuple-element.51) | data formatting | bytes 6553600 | tf_op jit(solution)/shard_map/dot_general | solution.py:102
  95.4 15.2 %all-gather.1 = bf16[1,1,1,128,2560]{4,3,2,1,0:T(8,128)(2,1)S(1)} all-gather(bf16[1,1,1,32,2560]{4,3,2,1,0:T(8,128)(2,1)S(1)} %copy-done.33), channel_id=3, replica_groups=mesh['section'=4,'tensor'=4,'dp'=2] {'tensor'}, dimensions={3}, use_global_device_ids=true | all-gather | bytes 819200 | tf_op jit(solution)/shard_map/all_gather | solution.py:101
  111.5 3.4 fusion.38
  123.0 4.0 convolution_convert_fusion.2
  129.2 4.0 convolution_convert_fusion.3
  137.2 13.4 %reduce-scatter.9.cloned.1.call-done = bf16[32,2560]{1,0:T(8,128)(2,1)} async-done(((bf16[128,2560]{1,0:T(8,128)(2,1)}), bf16[32,2560]{1,0:T(8,128)(2,1)}) %reduce-scatter.9.cloned.1.call-update) | async-done | bytes 163856 | tf_op jit(solution)/shard_map/reduce_scatter | solution.py:166
  150.5 24.1 %reduce-scatter.7.cloned.1.call-done = bf16[32,2560]{1,0:T(8,128)(2,1)} async-done(((bf16[128,2560]{1,0:T(8,128)(2,1)}), bf16[32,2560]{1,0:T(8,128)(2,1)}) %reduce-scatter.7.cloned.1.call-update) | async-done | bytes 163856 | tf_op jit(solution)/shard_map/reduce_scatter | solution.py:166
  178.8 16.5 %all_gather.30 = bf16[128,2560]{1,0:T(8,128)(2,1)S(1)} all-gather(bf16[32,2560]{1,0:T(8,128)(2,1)S(1)} %get-tuple-element.54), channel_id=1, replica_groups=mesh['section'=4,'tensor'=4,'dp'=2] {'tensor'}, dimensions={0}, use_global_device_ids=true | all-gather | bytes 819200 | tf_op jit(solution)/shard_map/all_gather | solution.py:100
  196.4 15.8 %all_gather.28 = bf16[128,2560]{1,0:T(8,128)(2,1)S(1)} all-gather(bf16[32,2560]{1,0:T(8,128)(2,1)S(1)} %get-tuple-element.55), channel_id=1, replica_groups=mesh['section'=4,'tensor'=4,'dp'=2] {'tensor'}, dimensions={0}, use_global_device_ids=true | all-gather | bytes 819200 | tf_op jit(solution)/shard_map/all_gather | solution.py:100
  221.0 17.3 %all_gather.29 = bf16[128,2560]{1,0:T(8,128)(2,1)S(1)} all-gather(bf16[32,2560]{1,0:T(8,128)(2,1)S(1)} %broadcast_select_fusion), channel_id=1, replica_groups=mesh['section'=4,'tensor'=4,'dp'=2] {'tensor'}, dimensions={0}, use_global_device_ids=true | all-gather | bytes 819200 | tf_op jit(solution)/shard_map/all_gather | solution.py:101
  244.0 16.7 %all_gather.31 = bf16[128,2560]{1,0:T(8,128)(2,1)S(1)} all-gather(bf16[32,2560]{1,0:T(8,128)(2,1)S(1)} %bitcast_select_fusion), channel_id=1, replica_groups=mesh['section'=4,'tensor'=4,'dp'=2] {'tensor'}, dimensions={0}, use_global_device_ids=true | all-gather | bytes 819200 | tf_op jit(solution)/shard_map/all_gather | solution.py:101
  261.5 3.5 fusion.41
  277.3 4.0 convolution_convert_fusion.1
  284.5 3.4 fusion.3
  298.0 3.4 pad_maximum_fusion
  302.5 19.2 %reduce-scatter.11.cloned.1.call-done = bf16[32,2560]{1,0:T(8,128)(2,1)} async-done(((bf16[128,2560]{1,0:T(8,128)(2,1)}), bf16[32,2560]{1,0:T(8,128)(2,1)}) %reduce-scatter.11.cloned.1.call-update) | async-done | bytes 163856 | tf_op jit(solution)/shard_map/reduce_scatter | solution.py:166
  323.2 36.0 %psum.7 = f32[2,1,2560]{2,1,0:T(1,128)} all-reduce(f32[2,1,2560]{2,1,0:T(1,128)S(1)} %broadcast_in_dim.33), channel_id=1, replica_groups=mesh['section'=4,'tensor'=4,'dp'=2] {'tensor','dp'}, use_global_device_ids=true, to_apply=%region_30.31 | all-reduce | flops 5120 | bytes 40960 | tf_op jit(solution)/shard_map/psum | solution.py:213
  361.4 28.5 %reduce-scatter.17.cloned.1.call-done = bf16[2,256,2560]{2,1,0:T(8,128)(2,1)} async-done(((bf16[2,512,2560]{2,1,0:T(8,128)(2,1)}), bf16[2,256,2560]{2,1,0:T(8,128)(2,1)}) %reduce-scatter.17.cloned.1.call-update) | async-done | bytes 2621456 | tf_op jit(solution)/shard_map/reduce_scatter | solution.py:209
  389.9 82.6 %reduce-scatter.15.cloned.1.call-done = bf16[2,1280,640]{2,1,0:T(8,128)(2,1)} async-done(((bf16[2,2560,640]{2,1,0:T(8,128)(2,1)}), bf16[2,1280,640]{2,1,0:T(8,128)(2,1)}) %reduce-scatter.15.cloned.1.call-update) | async-done | bytes 3276816 | tf_op jit(solution)/shard_map/reduce_scatter | solution.py:206
  (327 shorter events, 83.0 us)
Async XLA Ops:
  7.2 28.0 %copy-start.1 = (bf16[2,2,1,1,32,2560]{5,4,3,2,1,0:T(8,128)(2,1)S(1)}, bf16[2,2,1,1,32,2560]{5,4,3,2,1,0:T(8,128)(2,1)}, u32[]{:S(2)}) copy-start(bf16[2,2,1,1,32,2560]{5,4,3,2,1,0:T(8,128)(2,1)} %param.6) | copy-start | bytes 1966084
  7.2 143.4 %reduce-scatter.9.cloned.1.call-start = ((), (), s32[]{:S(2)}) async-start(), calls=%async_computation.7 | async-start | bytes 819200 | tf_op jit(solution)/shard_map/reduce_scatter | solution.py:166
  7.2 84.4 %copy-start.88 = (f32[32]{0:T(128)}, f32[32]{0:T(128)S(1)}, u32[]{:S(2)}) copy-start(f32[32]{0:T(128)S(1)} %negate_power_fusion) | copy-start | bytes 388
  7.3 85.9 %copy-start.49 = (pred[128,128]{0,1:T(8,128)(4,1)}, pred[128,128]{0,1:T(8,128)(4,1)S(1)}, u32[]{:S(2)}) copy-start(pred[128,128]{0,1:T(8,128)(4,1)S(1)} %iota_compare_fusion) | copy-start | bytes 49156
  10.1 82.3 %copy-start.45 = (f32[128,32]{0,1:T(8,128)}, f32[128,32]{0,1:T(8,128)S(1)}, u32[]{:S(2)}) copy-start(f32[128,32]{0,1:T(8,128)S(1)} %get-tuple-element.112) | copy-start | bytes 49156
  10.1 82.3 %copy-start.59 = (f32[128,32]{0,1:T(8,128)}, f32[128,32]{0,1:T(8,128)S(1)}, u32[]{:S(2)}) copy-start(f32[128,32]{0,1:T(8,128)S(1)} %get-tuple-element.111) | copy-start | bytes 49156
  35.1 58.4 %copy-start.63 = (bf16[128,512]{0,1:T(8,128)(2,1)}, bf16[128,512]{0,1:T(8,128)(2,1)S(1)}, u32[]{:S(2)}) copy-start(bf16[128,512]{0,1:T(8,128)(2,1)S(1)} %copy.40) | copy-start | bytes 393220
  35.2 40.7 %copy-start.92 = (f32[32]{0:T(128)}, f32[32]{0:T(128)S(1)}, u32[]{:S(2)}) copy-start(f32[32]{0:T(128)S(1)} %get-tuple-element.129) | copy-start | bytes 388
  35.2 40.7 %copy-start.94 = (f32[32]{0:T(128)}, f32[32]{0:T(128)S(1)}, u32[]{:S(2)}) copy-start(f32[32]{0:T(128)S(1)} %get-tuple-element.130) | copy-start | bytes 388
  127.0 47.6 %reduce-scatter.7.cloned.1.call-start = ((), (), s32[]{:S(2)}) async-start(), calls=%async_computation.6 | async-start | bytes 819200 | tf_op jit(solution)/shard_map/reduce_scatter | solution.py:166
  133.1 41.5 %copy-start.43 = (f32[2560]{0:T(1024)S(1)}, f32[2560]{0:T(1024)}, u32[]{:S(2)}) copy-start(f32[2560]{0:T(1024)} %copy-done.42) | copy-start | bytes 30724
  133.2 41.5 %copy-start.93 = (f32[32]{0:T(128)S(1)}, f32[32]{0:T(128)}, u32[]{:S(2)}) copy-start(f32[32]{0:T(128)} %copy-done.92) | copy-start | bytes 388
  133.2 41.5 %copy-start.95 = (f32[32]{0:T(128)S(1)}, f32[32]{0:T(128)}, u32[]{:S(2)}) copy-start(f32[32]{0:T(128)} %copy-done.94) | copy-start | bytes 388
  133.2 169.3 %reduce-scatter.13.cloned.1.call-start = ((), (), s32[]{:S(2)}) async-start(), calls=%async_computation.9 | async-start | bytes 819200 | tf_op jit(solution)/shard_map/reduce_scatter | solution.py:166
  178.8 34.6 %copy-start.31 = (bf16[32,2560]{1,0:T(8,128)(2,1)}, bf16[32,2560]{1,0:T(8,128)(2,1)S(1)}, u32[]{:S(2)}) copy-start(bf16[32,2560]{1,0:T(8,128)(2,1)S(1)} %get-tuple-element.52) | copy-start | bytes 491524
  178.8 41.5 %copy-start.19 = (bf16[32,2560]{1,0:T(8,128)(2,1)}, bf16[32,2560]{1,0:T(8,128)(2,1)S(1)}, u32[]{:S(2)}) copy-start(bf16[32,2560]{1,0:T(8,128)(2,1)S(1)} %get-tuple-element.53) | copy-start | bytes 491524
  195.3 43.9 %slice-start.2 = ((s8[5242880]{0:T(1024)(128)(4,1)}), s8[1048576]{0:T(1024)(128)(4,1)S(1)}, s32[]{:S(2)}) async-start(s8[5242880]{0:T(1024)(128)(4,1)} %bitcast.493), calls=%async_computation.14 | async-start | bytes 2097152
  213.4 6.9 %collective-permute-start.1 = (bf16[32,2560]{1,0:T(8,128)(2,1)S(1)}, bf16[32,2560]{1,0:T(8,128)(2,1)S(1)}, u32[]{:S(2)}, u32[]{:S(2)}) collective-permute-start(bf16[32,2560]{1,0:T(8,128)(2,1)S(1)} %get-tuple-element.52), channel_id=1, source_target_pairs={{8,0},{16,8},{24,16},{9,1},{17,9},{25,17},{10,2},{18,10},{26,18},{... | collective-permute-start | bytes 491528 | tf_op jit(solution)/shard_map/ppermute | solution.py:17
  214.8 5.5 %collective-permute-start = (bf16[32,2560]{1,0:T(8,128)(2,1)S(1)}, bf16[32,2560]{1,0:T(8,128)(2,1)S(1)}, u32[]{:S(2)}, u32[]{:S(2)}) collective-permute-start(bf16[32,2560]{1,0:T(8,128)(2,1)S(1)} %get-tuple-element.53), channel_id=1, source_target_pairs={{0,8},{8,16},{16,24},{1,9},{9,17},{17,25},{2,10},{10,18},{18,26},{... | collective-permute-start | bytes 491528 | tf_op jit(solution)/shard_map/ppermute | solution.py:17
  274.2 47.5 %reduce-scatter.11.cloned.1.call-start = ((), (), s32[]{:S(2)}) async-start(), calls=%async_computation.8 | async-start | bytes 819200 | tf_op jit(solution)/shard_map/reduce_scatter | solution.py:166
  284.4 105.5 %reduce-scatter.17.cloned.1.call-start = ((), (), s32[]{:S(2)}) async-start(), calls=%async_computation.11 | async-start | bytes 7864320 | tf_op jit(solution)/shard_map/reduce_scatter | solution.py:209
  292.6 179.9 %reduce-scatter.15.cloned.1.call-start = ((), (), s32[]{:S(2)}) async-start(), calls=%async_computation.10 | async-start | bytes 9830400 | tf_op jit(solution)/shard_map/reduce_scatter | solution.py:206
  301.5 57.7 %copy-start.22 = (bf16[32,2560]{1,0:T(8,128)(2,1)S(1)}, bf16[32,2560]{1,0:T(8,128)(2,1)}, u32[]{:S(2)}) copy-start(bf16[32,2560]{1,0:T(8,128)(2,1)} %copy-done.21) | copy-start | bytes 491524
  301.5 57.7 %copy-start.24 = (bf16[32,2560]{1,0:T(8,128)(2,1)S(1)}, bf16[32,2560]{1,0:T(8,128)(2,1)}, u32[]{:S(2)}) copy-start(bf16[32,2560]{1,0:T(8,128)(2,1)} %copy-done.23) | copy-start | bytes 491524
  (88 other events, 629.8 us)
Sparse Core Ops, SparseCore 0:
  127.1 23.3 reduce-scatter.8
  153.4 21.2 reduce-scatter.6
  274.4 23.2 reduce-scatter.12
  300.4 21.2 reduce-scatter.10
  324.4 65.4 reduce-scatter.16
  392.6 79.8 reduce-scatter.14
where the time goes:
time: 481 us; the launch traced here: 479 us
  blocking collectives  171 us (36%)
  waiting for transfers between devices  168 us (35%)
  matrix products  64 us (13%)
  local copies, waits for them, and re-layouts  32.3 us (7%)
  other arithmetic  23 us (5%)
  between operations  15.6 us (3%)
  starting transfers between devices  4.93 us (1%)
    reduce_scatter x1, waiting for transfers between devices, local(): lax.psum_scatter(jnp.stack(qkv_sums).astype(jnp.bfloat16), 'dp', scatter_...  82.6 us
    all_gather x4, blocking collectives, local(): input_grad_full = lax.all_gather(grad_output, 'tensor', axis=0, tiled=True)  68.9 us
    all_gather x4, blocking collectives, local(): input_normed = lax.all_gather(normed_own, 'tensor', axis=0, tiled=True)  66.6 us
    reduce_scatter x4, waiting for transfers between devices, local(): lax.psum_scatter(lax.dot_general(input_grad_projected, weight_qkv[member]...  56.8 us
    psum x1, blocking collectives, local(): gain_total = lax.psum(jnp.stack(gain_totals), ('tensor', 'dp'))  36 us
    reduce_scatter x1, waiting for transfers between devices, local(): lax.psum_scatter(jnp.stack(out_sums).astype(jnp.bfloat16), 'dp', scatter_...  28.5 us
    dot_general x3, local copies, waits for them, and re-layouts, local(): jnp.dot(input_normed, weight_qkv[member], preferred_element_type=jnp.floa...  15.9 us
    dot_general x4, matrix products, local(): lax.dot_general(input_grad_projected, weight_qkv[member], contract_cols,...  14 us
  transfers between devices with their start and end apart: 8, of which 5 were waited for; matrix products, arithmetic and copies ran while one was open for 8% of the time, Pallas kernels for 0%

commit v1 on v0

--- a/solution.py
+++ b/solution.py
@@ -210,7 +210,7 @@
             jnp.stack(out_sums).astype(jnp.bfloat16), "dp", scatter_dimension=1, tiled=True
         ).astype(jnp.float32),
     )
-    gain_total = lax.psum(jnp.stack(gain_totals), ("tensor", "dp"))
+    gain_total = jnp.sum(lax.all_gather(jnp.stack(gain_totals), ("tensor", "dp")), axis=0)
     unit_grads = jnp.stack(per_tick)[:, :, None, None]
     return (
         unit_grads,

time: 481 us -> 482 us (level)
  waiting for transfers between devices: 168 us -> 174 us
  blocking collectives: 171 us -> 166 us
    psum x1 -> x0, blocking collectives: 36 us -> none  [local(): gain_total = lax.psum(jnp.stack(gain_totals), ('tensor', 'dp'))]
    all_gather x0 -> x1, blocking collectives: none -> 31 us  [local(): lax.all_gather(jnp.stack(gain_totals), ('tensor', 'dp'))]
    reduce_scatter x1, waiting for transfers between devices: 28.5 us -> 34.1 us  [local(): lax.psum_scatter(jnp.stack(out_sums).astype(jnp.bfloat16), 'dp', scatter_...]
  transfers between devices with their start and end apart: 8 -> 8, of which waited for: 5 -> 5; matrix products, arithmetic and copies ran while one was open for 8% -> 9% of each run, Pallas kernels for 0% -> 0%
where the time goes in v1:
time: 482 us; the launch traced here: 481 us
  waiting for transfers between devices  174 us (36%)
  blocking collectives  166 us (34%)
  matrix products  64 us (13%)
  local copies, waits for them, and re-layouts  33 us (7%)
  other arithmetic  23.1 us (5%)
  between operations  15.6 us (3%)
  starting transfers between devices  4.93 us (1%)
    reduce_scatter x1, waiting for transfers between devices, local(): lax.psum_scatter(jnp.stack(qkv_sums).astype(jnp.bfloat16), 'dp', scatter_...  82.6 us
    all_gather x4, blocking collectives, local(): input_grad_full = lax.all_gather(grad_output, 'tensor', axis=0, tiled=True)  68.9 us
    all_gather x4, blocking collectives, local(): input_normed = lax.all_gather(normed_own, 'tensor', axis=0, tiled=True)  66.6 us
    reduce_scatter x4, waiting for transfers between devices, local(): lax.psum_scatter(lax.dot_general(input_grad_projected, weight_qkv[member]...  56.8 us
    reduce_scatter x1, waiting for transfers between devices, local(): lax.psum_scatter(jnp.stack(out_sums).astype(jnp.bfloat16), 'dp', scatter_...  34.1 us
    all_gather x1, blocking collectives, local(): lax.all_gather(jnp.stack(gain_totals), ('tensor', 'dp'))  31 us
    dot_general x3, local copies, waits for them, and re-layouts, local(): jnp.dot(input_normed, weight_qkv[member], preferred_element_type=jnp.floa...  15.9 us
    dot_general x4, matrix products, local(): lax.dot_general(input_grad_projected, weight_qkv[member], contract_cols,...  14 us
  transfers between devices with their start and end apart: 8, of which 5 were waited for; matrix products, arithmetic and copies ran while one was open for 9% of the time, Pallas kernels for 0%

profile of v1, /device:TPU:0, one launch (start us, length us, event | category | flops | bytes accessed | tf_op | source)
XLA Modules:
  0.0 480.7 jit_solution(13351605759696971080)
XLA Ops:
  11.8 19.7 %all-gather = bf16[1,1,1,128,2560]{4,3,2,1,0:T(8,128)(2,1)S(1)} all-gather(bf16[1,1,1,32,2560]{4,3,2,1,0:T(8,128)(2,1)S(1)} %get-tuple-element.72), channel_id=2, replica_groups=mesh['section'=4,'tensor'=4,'dp'=2] {'tensor'}, dimensions={3}, use_global_device_ids=true | all-gather | bytes 819200 | tf_op jit(solution)/shard_map/all_gather | solution.py:101
  35.4 17.5 %all_gather.30 = bf16[128,2560]{1,0:T(8,128)(2,1)} all-gather(bf16[32,2560]{1,0:T(8,128)(2,1)S(1)} %get-tuple-element.62), channel_id=1, replica_groups=mesh['section'=4,'tensor'=4,'dp'=2] {'tensor'}, dimensions={0}, use_global_device_ids=true | all-gather | bytes 819200 | tf_op jit(solution)/shard_map/all_gather | solution.py:100
  52.9 16.7 %all_gather.32 = bf16[128,2560]{1,0:T(8,128)(2,1)} all-gather(bf16[32,2560]{1,0:T(8,128)(2,1)S(1)} %get-tuple-element.63), channel_id=1, replica_groups=mesh['section'=4,'tensor'=4,'dp'=2] {'tensor'}, dimensions={0}, use_global_device_ids=true | all-gather | bytes 819200 | tf_op jit(solution)/shard_map/all_gather | solution.py:100
  69.6 6.2 %slice_bitcast_fusion.1 = (bf16[640,2560]{0,1:T(8,128)(2,1)}, bf16[640,2560]{0,1:T(8,128)(2,1)}) fusion(bf16[2,1,2560,640]{3,2,1,0:T(8,128)(2,1)} %param.9), kind=kLoop, calls=%fused_computation.30 | loop fusion | bytes 13107200 | tf_op jit(solution)/shard_map/dot_general | solution.py:102
  75.9 4.0 copy.64
  82.7 5.7 %copy.69 = bf16[640,2560]{1,0:T(8,128)(2,1)} copy(bf16[640,2560]{0,1:T(8,128)(2,1)} %get-tuple-element.55) | data formatting | bytes 6553600 | tf_op jit(solution)/shard_map/dot_general | solution.py:102
  95.4 15.2 %all-gather.1 = bf16[1,1,1,128,2560]{4,3,2,1,0:T(8,128)(2,1)S(1)} all-gather(bf16[1,1,1,32,2560]{4,3,2,1,0:T(8,128)(2,1)S(1)} %copy-done.33), channel_id=3, replica_groups=mesh['section'=4,'tensor'=4,'dp'=2] {'tensor'}, dimensions={3}, use_global_device_ids=true | all-gather | bytes 819200 | tf_op jit(solution)/shard_map/all_gather | solution.py:101
  111.5 3.4 fusion.38
  123.0 4.0 convolution_convert_fusion.2
  129.2 4.0 convolution_convert_fusion.3
  137.2 13.4 %reduce-scatter.9.cloned.1.call-done = bf16[32,2560]{1,0:T(8,128)(2,1)} async-done(((bf16[128,2560]{1,0:T(8,128)(2,1)}), bf16[32,2560]{1,0:T(8,128)(2,1)}) %reduce-scatter.9.cloned.1.call-update) | async-done | bytes 163856 | tf_op jit(solution)/shard_map/reduce_scatter | solution.py:166
  150.5 24.1 %reduce-scatter.7.cloned.1.call-done = bf16[32,2560]{1,0:T(8,128)(2,1)} async-done(((bf16[128,2560]{1,0:T(8,128)(2,1)}), bf16[32,2560]{1,0:T(8,128)(2,1)}) %reduce-scatter.7.cloned.1.call-update) | async-done | bytes 163856 | tf_op jit(solution)/shard_map/reduce_scatter | solution.py:166
  178.8 16.5 %all_gather.36 = bf16[128,2560]{1,0:T(8,128)(2,1)S(1)} all-gather(bf16[32,2560]{1,0:T(8,128)(2,1)S(1)} %get-tuple-element.58), channel_id=1, replica_groups=mesh['section'=4,'tensor'=4,'dp'=2] {'tensor'}, dimensions={0}, use_global_device_ids=true | all-gather | bytes 819200 | tf_op jit(solution)/shard_map/all_gather | solution.py:100
  196.4 15.8 %all_gather.34 = bf16[128,2560]{1,0:T(8,128)(2,1)S(1)} all-gather(bf16[32,2560]{1,0:T(8,128)(2,1)S(1)} %get-tuple-element.59), channel_id=1, replica_groups=mesh['section'=4,'tensor'=4,'dp'=2] {'tensor'}, dimensions={0}, use_global_device_ids=true | all-gather | bytes 819200 | tf_op jit(solution)/shard_map/all_gather | solution.py:100
  221.0 17.3 %all_gather.35 = bf16[128,2560]{1,0:T(8,128)(2,1)S(1)} all-gather(bf16[32,2560]{1,0:T(8,128)(2,1)S(1)} %broadcast_select_fusion), channel_id=1, replica_groups=mesh['section'=4,'tensor'=4,'dp'=2] {'tensor'}, dimensions={0}, use_global_device_ids=true | all-gather | bytes 819200 | tf_op jit(solution)/shard_map/all_gather | solution.py:101
  244.0 16.7 %all_gather.37 = bf16[128,2560]{1,0:T(8,128)(2,1)S(1)} all-gather(bf16[32,2560]{1,0:T(8,128)(2,1)S(1)} %bitcast_select_fusion), channel_id=1, replica_groups=mesh['section'=4,'tensor'=4,'dp'=2] {'tensor'}, dimensions={0}, use_global_device_ids=true | all-gather | bytes 819200 | tf_op jit(solution)/shard_map/all_gather | solution.py:101
  261.5 3.5 fusion.41
  277.3 4.0 convolution_convert_fusion.1
  284.5 3.4 fusion.3
  298.0 3.4 pad_maximum_fusion
  302.5 19.2 %reduce-scatter.11.cloned.1.call-done = bf16[32,2560]{1,0:T(8,128)(2,1)} async-done(((bf16[128,2560]{1,0:T(8,128)(2,1)}), bf16[32,2560]{1,0:T(8,128)(2,1)}) %reduce-scatter.11.cloned.1.call-update) | async-done | bytes 163856 | tf_op jit(solution)/shard_map/reduce_scatter | solution.py:166
  323.2 31.0 %all-gather.3 = f32[8,2,2560]{2,1,0:T(2,128)S(1)} all-gather(f32[1,2,2560]{2,1,0:T(2,128)S(1)} %maximum_bitcast_fusion.7), channel_id=4, replica_groups=mesh['section'=4,'tensor'=4,'dp'=2] {'tensor','dp'}, dimensions={0}, use_global_device_ids=true | all-gather | bytes 184320 | tf_op jit(solution)/shard_map/all_gather | solution.py:213
  357.1 34.1 %reduce-scatter.17.cloned.1.call-done = bf16[2,256,2560]{2,1,0:T(8,128)(2,1)} async-done(((bf16[2,512,2560]{2,1,0:T(8,128)(2,1)}), bf16[2,256,2560]{2,1,0:T(8,128)(2,1)}) %reduce-scatter.17.cloned.1.call-update) | async-done | bytes 2621456 | tf_op jit(solution)/shard_map/reduce_scatter | solution.py:209
  391.2 82.6 %reduce-scatter.15.cloned.1.call-done = bf16[2,1280,640]{2,1,0:T(8,128)(2,1)} async-done(((bf16[2,2560,640]{2,1,0:T(8,128)(2,1)}), bf16[2,1280,640]{2,1,0:T(8,128)(2,1)}) %reduce-scatter.15.cloned.1.call-update) | async-done | bytes 3276816 | tf_op jit(solution)/shard_map/reduce_scatter | solution.py:206
  (328 shorter events, 83.7 us)
Async XLA Ops:
  7.2 28.0 %copy-start.1 = (bf16[2,2,1,1,32,2560]{5,4,3,2,1,0:T(8,128)(2,1)S(1)}, bf16[2,2,1,1,32,2560]{5,4,3,2,1,0:T(8,128)(2,1)}, u32[]{:S(2)}) copy-start(bf16[2,2,1,1,32,2560]{5,4,3,2,1,0:T(8,128)(2,1)} %param.6) | copy-start | bytes 1966084
  7.2 143.4 %reduce-scatter.9.cloned.1.call-start = ((), (), s32[]{:S(2)}) async-start(), calls=%async_computation.7 | async-start | bytes 819200 | tf_op jit(solution)/shard_map/reduce_scatter | solution.py:166
  7.2 84.4 %copy-start.88 = (f32[32]{0:T(128)}, f32[32]{0:T(128)S(1)}, u32[]{:S(2)}) copy-start(f32[32]{0:T(128)S(1)} %negate_power_fusion) | copy-start | bytes 388
  7.3 85.9 %copy-start.49 = (pred[128,128]{0,1:T(8,128)(4,1)}, pred[128,128]{0,1:T(8,128)(4,1)S(1)}, u32[]{:S(2)}) copy-start(pred[128,128]{0,1:T(8,128)(4,1)S(1)} %iota_compare_fusion) | copy-start | bytes 49156
  10.1 82.3 %copy-start.45 = (f32[128,32]{0,1:T(8,128)}, f32[128,32]{0,1:T(8,128)S(1)}, u32[]{:S(2)}) copy-start(f32[128,32]{0,1:T(8,128)S(1)} %get-tuple-element.116) | copy-start | bytes 49156
  10.1 82.3 %copy-start.59 = (f32[128,32]{0,1:T(8,128)}, f32[128,32]{0,1:T(8,128)S(1)}, u32[]{:S(2)}) copy-start(f32[128,32]{0,1:T(8,128)S(1)} %get-tuple-element.115) | copy-start | bytes 49156
  35.1 58.4 %copy-start.63 = (bf16[128,512]{0,1:T(8,128)(2,1)}, bf16[128,512]{0,1:T(8,128)(2,1)S(1)}, u32[]{:S(2)}) copy-start(bf16[128,512]{0,1:T(8,128)(2,1)S(1)} %copy.65) | copy-start | bytes 393220
  35.2 40.7 %copy-start.92 = (f32[32]{0:T(128)}, f32[32]{0:T(128)S(1)}, u32[]{:S(2)}) copy-start(f32[32]{0:T(128)S(1)} %get-tuple-element.133) | copy-start | bytes 388
  35.2 40.7 %copy-start.94 = (f32[32]{0:T(128)}, f32[32]{0:T(128)S(1)}, u32[]{:S(2)}) copy-start(f32[32]{0:T(128)S(1)} %get-tuple-element.134) | copy-start | bytes 388
  127.0 47.6 %reduce-scatter.7.cloned.1.call-start = ((), (), s32[]{:S(2)}) async-start(), calls=%async_computation.6 | async-start | bytes 819200 | tf_op jit(solution)/shard_map/reduce_scatter | solution.py:166
  133.1 41.5 %copy-start.43 = (f32[2560]{0:T(1024)S(1)}, f32[2560]{0:T(1024)}, u32[]{:S(2)}) copy-start(f32[2560]{0:T(1024)} %copy-done.42) | copy-start | bytes 30724
  133.2 41.5 %copy-start.93 = (f32[32]{0:T(128)S(1)}, f32[32]{0:T(128)}, u32[]{:S(2)}) copy-start(f32[32]{0:T(128)} %copy-done.92) | copy-start | bytes 388
  133.2 41.5 %copy-start.95 = (f32[32]{0:T(128)S(1)}, f32[32]{0:T(128)}, u32[]{:S(2)}) copy-start(f32[32]{0:T(128)} %copy-done.94) | copy-start | bytes 388
  133.2 169.3 %reduce-scatter.13.cloned.1.call-start = ((), (), s32[]{:S(2)}) async-start(), calls=%async_computation.9 | async-start | bytes 819200 | tf_op jit(solution)/shard_map/reduce_scatter | solution.py:166
  178.8 34.6 %copy-start.31 = (bf16[32,2560]{1,0:T(8,128)(2,1)}, bf16[32,2560]{1,0:T(8,128)(2,1)S(1)}, u32[]{:S(2)}) copy-start(bf16[32,2560]{1,0:T(8,128)(2,1)S(1)} %get-tuple-element.56) | copy-start | bytes 491524
  178.8 41.5 %copy-start.19 = (bf16[32,2560]{1,0:T(8,128)(2,1)}, bf16[32,2560]{1,0:T(8,128)(2,1)S(1)}, u32[]{:S(2)}) copy-start(bf16[32,2560]{1,0:T(8,128)(2,1)S(1)} %get-tuple-element.57) | copy-start | bytes 491524
  195.3 43.9 %slice-start.2 = ((s8[5242880]{0:T(1024)(128)(4,1)}), s8[1048576]{0:T(1024)(128)(4,1)S(1)}, s32[]{:S(2)}) async-start(s8[5242880]{0:T(1024)(128)(4,1)} %bitcast.495), calls=%async_computation.14 | async-start | bytes 2097152
  213.4 6.9 %collective-permute-start.1 = (bf16[32,2560]{1,0:T(8,128)(2,1)S(1)}, bf16[32,2560]{1,0:T(8,128)(2,1)S(1)}, u32[]{:S(2)}, u32[]{:S(2)}) collective-permute-start(bf16[32,2560]{1,0:T(8,128)(2,1)S(1)} %get-tuple-element.56), channel_id=1, source_target_pairs={{8,0},{16,8},{24,16},{9,1},{17,9},{25,17},{10,2},{18,10},{26,18},{... | collective-permute-start | bytes 491528 | tf_op jit(solution)/shard_map/ppermute | solution.py:17
  214.8 5.5 %collective-permute-start = (bf16[32,2560]{1,0:T(8,128)(2,1)S(1)}, bf16[32,2560]{1,0:T(8,128)(2,1)S(1)}, u32[]{:S(2)}, u32[]{:S(2)}) collective-permute-start(bf16[32,2560]{1,0:T(8,128)(2,1)S(1)} %get-tuple-element.57), channel_id=1, source_target_pairs={{0,8},{8,16},{16,24},{1,9},{9,17},{17,25},{2,10},{10,18},{18,26},{... | collective-permute-start | bytes 491528 | tf_op jit(solution)/shard_map/ppermute | solution.py:17
  274.2 47.5 %reduce-scatter.11.cloned.1.call-start = ((), (), s32[]{:S(2)}) async-start(), calls=%async_computation.8 | async-start | bytes 819200 | tf_op jit(solution)/shard_map/reduce_scatter | solution.py:166
  284.4 106.8 %reduce-scatter.17.cloned.1.call-start = ((), (), s32[]{:S(2)}) async-start(), calls=%async_computation.11 | async-start | bytes 7864320 | tf_op jit(solution)/shard_map/reduce_scatter | solution.py:209
  292.6 181.2 %reduce-scatter.15.cloned.1.call-start = ((), (), s32[]{:S(2)}) async-start(), calls=%async_computation.10 | async-start | bytes 9830400 | tf_op jit(solution)/shard_map/reduce_scatter | solution.py:206
  301.5 53.4 %copy-start.22 = (bf16[32,2560]{1,0:T(8,128)(2,1)S(1)}, bf16[32,2560]{1,0:T(8,128)(2,1)}, u32[]{:S(2)}) copy-start(bf16[32,2560]{1,0:T(8,128)(2,1)} %copy-done.21) | copy-start | bytes 491524
  301.5 53.4 %copy-start.24 = (bf16[32,2560]{1,0:T(8,128)(2,1)S(1)}, bf16[32,2560]{1,0:T(8,128)(2,1)}, u32[]{:S(2)}) copy-start(bf16[32,2560]{1,0:T(8,128)(2,1)} %copy-done.23) | copy-start | bytes 491524
  (88 other events, 629.8 us)
Sparse Core Ops, SparseCore 0:
  127.1 23.3 reduce-scatter.8
  153.4 21.2 reduce-scatter.6
  274.4 23.2 reduce-scatter.12
  300.4 21.2 reduce-scatter.10
  324.4 66.7 reduce-scatter.16
  393.9 79.8 reduce-scatter.14
